TPU v7x, 32 devices: a whole 2x2x4 slice. The times are simulated.
32 devices in a mesh: row: 8 (over z, y), col: 4 (over x, core).
Axes of the slice: x: 2, y: 2, z: 4, core: 2. Of those that a mesh axis runs over, the one named last changes fastest.
Arguments:
- matrix: float32 [4096, 4096], P('row', 'col'), may hold values from -0.92 to 1.92, as said below
Outputs:
- inverse: float32 [4096, 4096], P('row', 'col')
- residual_norms: float32 [4], replicated
Inputs may be any that keep to these rules, and one draw needn't show every extreme that they name: matrix is exactly symmetric and positive definite; all its eigenvalues lie between 0.08 and 1.92.
All inputs are finite; a program needn't handle non-finite values.
Results may differ from a plain program's by a relative error of at most 0.0017.
The roundings to bfloat16 on the way count: a program that leaves them out, or rounds other values in their place, can miss the bound.
Values may be sent and summed in bfloat16 or wider, within the bound.
A program may use at most 64 MiB of HBM per device.

v0:
```python
import jax
import jax.numpy as jnp
from jax import lax
from jax.sharding import PartitionSpec as P

ITERS = 4


def rounded(value):
    return lax.reduce_precision(value, 8, 7)


def first_iterate(panel, scale_low, row_start, col_start):
    rows = row_start + lax.broadcasted_iota(jnp.int32, panel.shape, 0)
    cols = col_start + lax.broadcasted_iota(jnp.int32, panel.shape, 1)
    eye = (rows == cols).astype(jnp.float32)
    shift = rounded(eye + (eye - scale_low * panel.astype(jnp.float32)))
    return (scale_low * shift).astype(jnp.bfloat16)


def transpose_blocks(block, row_size, col_size):
    ratio = row_size // col_size
    side = block.shape[0]
    row_index = lax.axis_index("row")
    pieces = []
    for turn in range(ratio):
        pairs = []
        for row in range(row_size):
            for col in range(col_size):
                target_row = ratio * col + (row + turn) % ratio
                pairs.append((row * col_size + col, target_row * col_size + row // ratio))
        half = lax.rem(row_index + turn, ratio)
        piece = lax.dynamic_slice_in_dim(block, half * side, side, axis=1)
        pieces.append(lax.ppermute(piece, ("row", "col"), pairs).T)
    out = jnp.zeros_like(block)
    for turn in range(ratio):
        half = lax.rem(row_index - turn + ratio, ratio)
        out = lax.dynamic_update_slice_in_dim(out, pieces[turn], half * side, axis=1)
    return out


def shards(matrix):
    row_count, col_count = matrix.shape
    row_size, col_size = (lax.axis_size("row"), lax.axis_size("col"))
    order = col_count * col_size
    row_start = lax.axis_index("row") * row_count
    col_start = lax.axis_index("col") * col_count
    global_rows = row_start + lax.broadcasted_iota(jnp.int32, (row_count, col_count), 0)
    global_cols = col_start + lax.broadcasted_iota(jnp.int32, (row_count, col_count), 1)
    eye_block = (global_rows == global_cols).astype(jnp.float32)
    mat_low = matrix.astype(jnp.bfloat16)
    sq_total = lax.psum(jnp.sum(matrix * matrix), ("row", "col"))
    panel_rows = lax.all_gather(mat_low, "col", axis=1, tiled=True)
    panel_cols = lax.all_gather(mat_low, "row", axis=0, tiled=True)
    start_scale = jnp.sqrt(jnp.float32(order)) / jnp.sqrt(sq_total)
    scale_low = rounded(start_scale)
    residual = eye_block - scale_low * rounded(matrix)
    partial_list = [jnp.sum(residual * residual)]
    iterate_rows = first_iterate(panel_rows, scale_low, row_start, 0)
    iterate_cols = first_iterate(panel_cols, scale_low, 0, col_start)
    for iteration in range(1, ITERS):
        product = jnp.dot(iterate_rows, panel_cols, preferred_element_type=jnp.float32)
        residual = eye_block - product
        partial_list.append(jnp.sum(residual * residual))
        shift_low = (eye_block + residual).astype(jnp.bfloat16)
        current = jnp.dot(
            lax.all_gather(shift_low, "col", axis=1, tiled=True),
            iterate_cols,
            preferred_element_type=jnp.float32,
        )
        if iteration < ITERS - 1:
            cur_low = current.astype(jnp.bfloat16)
            iterate_rows = lax.all_gather(cur_low, "col", axis=1, tiled=True)
            iterate_cols = lax.all_gather(cur_low, "row", axis=0, tiled=True)
    summed = lax.psum(jnp.stack(partial_list), ("row", "col"))
    residual_norms = jnp.sqrt(summed / order)
    return (transpose_blocks(current, row_size, col_size), residual_norms)


def solution(mesh):
    in_specs = (P("row", "col"),)
    out_specs = (P("row", "col"), P())
    return jax.shard_map(shards, mesh=mesh, in_specs=in_specs, out_specs=out_specs, check_vma=False)
```

profile of v0, /device:TPU:0, one launch (start us, length us, event | category | flops | bytes accessed | tf_op | source)
XLA Modules:
  0.0 790.7 jit_solution(10998236796299218012)
XLA Ops:
  7.2 0.0 all-gather.10.cloned.1.call-start
  7.2 4.3 multiply_reduce_fusion.3
  11.5 0.0 all-gather.10.cloned.1.call-update
  11.5 0.0 all-gather.12.cloned.1.call-start
  11.5 0.7 all-gather.12.cloned.1.call-update
  12.3 0.0 all-gather.14.cloned.1.call-start
  12.3 42.5 %psum.14 = f32[]{:T(128)} all-reduce(f32[]{:T(128)} %get-tuple-element.9), channel_id=1, replica_groups=mesh['row'=8,'col'=4] {'row','col'}, use_global_device_ids=true, to_apply=%region_1.0 | all-reduce | flops 1 | bytes 8 | tf_op jit(solution)/shard_map/psum | solution.py:52
  56.0 0.0 all-gather.10.cloned.1.call-done
  56.0 120.3 %all-gather.12.cloned.1.call-done = bf16[4096,1024]{1,0:T(8,128)(2,1)} async-done(((bf16[512,1024]{1,0:T(8,128)(2,1)}), bf16[4096,1024]{1,0:T(8,128)(2,1)}) %all-gather.12.cloned.1.call-update) | async-done | bytes 8388624 | tf_op jit(solution)/shard_map/all_gather | solution.py:54
  176.3 12.1 %fusion.12 = (bf16[512,1024]{1,0:T(8,128)(2,1)}, f32[512,1024]{1,0:T(8,128)}) fusion(s32[1024]{0:T(1024)S(1)} %iota_add_fusion, s32[512]{0:T(512)S(1)} %iota_add_fusion.1, bf16[4096,1024]{1,0:T(8,128)(2,1)} %all-gather.12.cloned.1.call-done, bf16[512,4096]{1,0:T(8,128)(2,1)} %all-gather.10.cloned.1.call-done, f32[]{:T(128)} %reduce_precision.12), kind=kOutput, calls=%fused_computation.21 | convolution fusion | flops 4316463104 | bytes 15734788 | tf_op jit(solution)/shard_map/dot_general | solution.py:62
  188.4 0.0 all-gather.14.cloned.1.call-update
  188.5 0.0 all-gather.16.cloned.1.call-start
  188.5 32.7 %all-gather.14.cloned.1.call-done = bf16[512,4096]{1,0:T(8,128)(2,1)} async-done(((bf16[512,1024]{1,0:T(8,128)(2,1)}), bf16[512,4096]{1,0:T(8,128)(2,1)}) %all-gather.14.cloned.1.call-update) | async-done | bytes 4194320 | tf_op jit(solution)/shard_map/all_gather | solution.py:67
  221.3 12.0 %fusion.17 = bf16[512,1024]{1,0:T(8,128)(2,1)} fusion(bf16[512,4096]{1,0:T(8,128)(2,1)} %all-gather.14.cloned.1.call-done, bf16[4096,1024]{1,0:T(8,128)(2,1)} %all-gather.12.cloned.1.call-done, s32[1024]{0:T(1024)S(1)} %iota_add_fusion, f32[]{:T(128)} %reduce_precision.12), kind=kOutput, calls=%fused_computation.30 | convolution fusion | flops 4333240320 | bytes 13635588 | tf_op jit(solution)/shard_map/dot_general | solution.py:66
  233.2 0.0 all-gather.16.cloned.1.call-update
  233.3 0.2 all-gather.18.cloned.1.call-start
  233.5 34.4 %all-gather.16.cloned.1.call-done = bf16[512,4096]{1,0:T(8,128)(2,1)} async-done(((bf16[512,1024]{1,0:T(8,128)(2,1)}), bf16[512,4096]{1,0:T(8,128)(2,1)}) %all-gather.16.cloned.1.call-update) | async-done | bytes 4194320 | tf_op jit(solution)/shard_map/all_gather | solution.py:73
  267.9 10.9 %fusion.13 = (bf16[512,1024]{1,0:T(8,128)(2,1)}, f32[512,1024]{1,0:T(8,128)}) fusion(s32[1024]{0:T(1024)S(1)} %iota_add_fusion, s32[512]{0:T(512)S(1)} %iota_add_fusion.1, bf16[512,4096]{1,0:T(8,128)(2,1)} %all-gather.16.cloned.1.call-done, bf16[4096,1024]{1,0:T(8,128)(2,1)} %all-gather.12.cloned.1.call-done), kind=kOutput, calls=%fused_computation.22 | convolution fusion | flops 4297588736 | bytes 15734784 | tf_op jit(solution)/shard_map/dot_general | solution.py:62
  278.7 0.0 all-gather.18.cloned.1.call-update
  278.8 0.0 all-gather.20.cloned.1.call-start
  278.8 0.5 all-gather.20.cloned.1.call-update
  279.3 0.0 copy-start.1
  279.4 0.0 all-gather.22.cloned.1.call-start
  279.4 34.0 %all-gather.18.cloned.1.call-done = bf16[512,4096]{1,0:T(8,128)(2,1)} async-done(((bf16[512,1024]{1,0:T(8,128)(2,1)}), bf16[512,4096]{1,0:T(8,128)(2,1)}) %all-gather.18.cloned.1.call-update) | async-done | bytes 4194320 | tf_op jit(solution)/shard_map/all_gather | solution.py:67
  313.4 126.5 %all-gather.20.cloned.1.call-done = bf16[4096,1024]{1,0:T(8,128)(2,1)} async-done(((bf16[512,1024]{1,0:T(8,128)(2,1)}), bf16[4096,1024]{1,0:T(8,128)(2,1)}) %all-gather.20.cloned.1.call-update) | async-done | bytes 8388624 | tf_op jit(solution)/shard_map/all_gather | solution.py:74
  439.9 10.2 %convolution_convert_fusion = bf16[512,1024]{1,0:T(8,128)(2,1)} fusion(bf16[512,4096]{1,0:T(8,128)(2,1)} %all-gather.18.cloned.1.call-done, bf16[4096,1024]{1,0:T(8,128)(2,1)} %all-gather.20.cloned.1.call-done), kind=kOutput, calls=%fused_computation.31 | convolution fusion | flops 4295491584 | bytes 13631488 | tf_op jit(solution)/shard_map/dot_general | solution.py:66
  450.0 0.0 all-gather.22.cloned.1.call-update
  450.1 0.0 all-gather.24.cloned.1.call-start
  450.1 32.7 %all-gather.22.cloned.1.call-done = bf16[512,4096]{1,0:T(8,128)(2,1)} async-done(((bf16[512,1024]{1,0:T(8,128)(2,1)}), bf16[512,4096]{1,0:T(8,128)(2,1)}) %all-gather.22.cloned.1.call-update) | async-done | bytes 4194320 | tf_op jit(solution)/shard_map/all_gather | solution.py:73
  482.8 0.0 copy-done.1
  482.8 13.2 %fusion.16 = (f32[]{:T(128)}, f32[]{:T(128)}, f32[]{:T(128)}, f32[]{:T(128)}, bf16[512,1024]{1,0:T(8,128)(2,1)}) fusion(f32[512,1024]{1,0:T(8,128)S(1)} %copy-done.1, f32[]{:T(128)} %reduce_precision.12, s32[1024]{0:T(1024)S(1)} %iota_add_fusion, s32[512]{0:T(512)S(1)} %iota_add_fusion.1, f32[512,1024]{1,0:T(8,128)} %get-tuple-element.14, ...), kind=kOutput, calls=%fused_computation.25 | convolution fusion | flops 4304404480 | bytes 19929108 | tf_op jit(solution)/shard_map/dot_general | solution.py:62
  496.0 0.0 all-gather.24.cloned.1.call-update
  496.0 0.3 all-gather.26.cloned.1.call-start
  496.3 0.5 all-gather.26.cloned.1.call-update
  496.8 33.9 %all-gather.24.cloned.1.call-done = bf16[512,4096]{1,0:T(8,128)(2,1)} async-done(((bf16[512,1024]{1,0:T(8,128)(2,1)}), bf16[512,4096]{1,0:T(8,128)(2,1)}) %all-gather.24.cloned.1.call-update) | async-done | bytes 4194320 | tf_op jit(solution)/shard_map/all_gather | solution.py:67
  530.6 126.6 %all-gather.26.cloned.1.call-done = bf16[4096,1024]{1,0:T(8,128)(2,1)} async-done(((bf16[512,1024]{1,0:T(8,128)(2,1)}), bf16[4096,1024]{1,0:T(8,128)(2,1)}) %all-gather.26.cloned.1.call-update) | async-done | bytes 8388624 | tf_op jit(solution)/shard_map/all_gather | solution.py:74
  657.3 8.1 %fusion.20 = f32[512,1024]{1,0:T(8,128)S(1)} fusion(bf16[512,4096]{1,0:T(8,128)(2,1)} %all-gather.24.cloned.1.call-done, bf16[4096,1024]{1,0:T(8,128)(2,1)} %all-gather.26.cloned.1.call-done), kind=kOutput, calls=%fused_computation.40 | convolution fusion | flops 4294967296 | bytes 14680064 | tf_op jit(solution)/shard_map/dot_general | solution.py:66
  665.4 0.2 constant_dynamic-slice_fusion
  665.7 1.6 collective-permute-start
  667.3 0.6 collective-permute-start.1
  667.8 2.5 pad_maximum_fusion
  670.4 109.5 %psum.15 = f32[4]{0:T(128)S(1)} all-reduce(f32[4]{0:T(128)S(1)} %pad_maximum_fusion), channel_id=1, replica_groups=mesh['row'=8,'col'=4] {'row','col'}, use_global_device_ids=true, to_apply=%region_6.0 | all-reduce | flops 4 | bytes 32 | tf_op jit(solution)/shard_map/psum | solution.py:75
  779.9 0.5 multiply_sqrt_fusion
  780.4 0.0 collective-permute-done
  780.4 1.6 copy.3
  782.0 0.0 collective-permute-done.1
  782.0 0.3 copy.4
  782.4 0.2 broadcast_in_dim.3
  782.6 0.1 constant_dynamic-update-slice_fusion.1
  782.7 0.1 constant_dynamic-update-slice_fusion
  782.8 0.0 copy-start
  782.8 1.3 copy-done
  (2 shorter events, 0.0 us)
Async XLA Ops:
  7.2 48.9 %all-gather.10.cloned.1.call-start = ((), (), s32[]{:S(2)}) async-start(), calls=%async_computation | async-start | bytes 5242880 | tf_op jit(solution)/shard_map/all_gather | solution.py:53
  11.5 164.8 %all-gather.12.cloned.1.call-start = ((), (), s32[]{:S(2)}) async-start(), calls=%async_computation.1 | async-start | bytes 9437184 | tf_op jit(solution)/shard_map/all_gather | solution.py:54
  12.3 209.0 %all-gather.14.cloned.1.call-start = ((), (), s32[]{:S(2)}) async-start(), calls=%async_computation.2 | async-start | bytes 5242880 | tf_op jit(solution)/shard_map/all_gather | solution.py:67
  188.5 79.4 %all-gather.16.cloned.1.call-start = ((), (), s32[]{:S(2)}) async-start(), calls=%async_computation.3 | async-start | bytes 5242880 | tf_op jit(solution)/shard_map/all_gather | solution.py:73
  233.3 80.1 %all-gather.18.cloned.1.call-start = ((), (), s32[]{:S(2)}) async-start(), calls=%async_computation.4 | async-start | bytes 5242880 | tf_op jit(solution)/shard_map/all_gather | solution.py:67
  278.8 161.1 %all-gather.20.cloned.1.call-start = ((), (), s32[]{:S(2)}) async-start(), calls=%async_computation.5 | async-start | bytes 9437184 | tf_op jit(solution)/shard_map/all_gather | solution.py:74
  279.3 203.5 %copy-start.1 = (f32[512,1024]{1,0:T(8,128)S(1)}, f32[512,1024]{1,0:T(8,128)}, u32[]{:S(2)}) copy-start(f32[512,1024]{1,0:T(8,128)} %param.1) | copy-start | bytes 6291460
  279.4 203.5 %all-gather.22.cloned.1.call-start = ((), (), s32[]{:S(2)}) async-start(), calls=%async_computation.6 | async-start | bytes 5242880 | tf_op jit(solution)/shard_map/all_gather | solution.py:73
  450.1 80.6 %all-gather.24.cloned.1.call-start = ((), (), s32[]{:S(2)}) async-start(), calls=%async_computation.7 | async-start | bytes 5242880 | tf_op jit(solution)/shard_map/all_gather | solution.py:67
  496.0 161.3 %all-gather.26.cloned.1.call-start = ((), (), s32[]{:S(2)}) async-start(), calls=%async_computation.8 | async-start | bytes 9437184 | tf_op jit(solution)/shard_map/all_gather | solution.py:74
  665.7 114.8 %collective-permute-start = (f32[512,512]{1,0:T(8,128)S(1)}, f32[512,512]{1,0:T(8,128)}, u32[]{:S(2)}, u32[]{:S(2)}) collective-permute-start(f32[512,512]{1,0:T(8,128)S(1)} %get-tuple-element.8), channel_id=1, source_target_pairs={{0,0},{1,8},{2,16},{3,24},{4,4},{5,12},{6,20},{7,28},{8,1},{9,9},{... | collective-permute-start | bytes 3145736 | tf_op jit(solution)/shard_map/ppermute | solution.py:34
  667.3 114.7 %collective-permute-start.1 = (f32[512,512]{1,0:T(8,128)S(1)}, f32[512,512]{1,0:T(8,128)S(1)}, u32[]{:S(2)}, u32[]{:S(2)}) collective-permute-start(f32[512,512]{1,0:T(8,128)S(1)} %get-tuple-element.7), channel_id=1, source_target_pairs={{0,4},{1,12},{2,20},{3,28},{4,0},{5,8},{6,16},{7,24},{8,5},{9,13},... | collective-permute-start | bytes 3145736 | tf_op jit(solution)/shard_map/ppermute | solution.py:34
  782.8 1.3 copy-start
Sparse Core Ops, SparseCore 0:
  11.6 37.4 all-gather.9
  51.8 124.4 all-gather.11
  188.6 32.6 all-gather.13
  233.4 34.4 all-gather.15
  278.9 34.4 all-gather.17
  315.4 124.4 all-gather.19
  450.2 32.6 all-gather.21
  496.1 34.4 all-gather.23
  532.8 124.4 all-gather.25
where the time goes:
time: 791 us
  waiting for transfers between devices  543 us (69%)
  blocking collectives  152 us (19%)
  matrix products  66.4 us (8%)
  between operations  15.1 us (2%)
    all_gather x2, waiting for transfers between devices, shards(): iterate_cols = lax.all_gather(cur_low, 'row', axis=0, tiled=True)  253 us
    all_gather x1, waiting for transfers between devices, shards(): panel_cols = lax.all_gather(mat_low, 'row', axis=0, tiled=True)  120 us
    psum x1, blocking collectives, shards(): summed = lax.psum(jnp.stack(partial_list), ('row', 'col'))  110 us
    all_gather x3, waiting for transfers between devices, shards(): lax.all_gather(shift_low, 'col', axis=1, tiled=True)  101 us
    all_gather x2, waiting for transfers between devices, shards(): iterate_rows = lax.all_gather(cur_low, 'col', axis=1, tiled=True)  67.1 us
    psum x1, blocking collectives, shards(): sq_total = lax.psum(jnp.sum(matrix * matrix), ('row', 'col'))  42.5 us
    dot_general x3, matrix products, shards(): jnp.dot(iterate_rows, panel_cols, preferred_element_type=jnp.float32)  36.2 us
    dot_general x3, matrix products, shards(): jnp.dot(lax.all_gather(shift_low, 'col', axis=1, tiled=True), iterate_col...  30.3 us
  transfers between devices with their start and end apart: 11, of which 8 were waited for; matrix products, arithmetic and copies ran while one was open for 1% of the time, Pallas kernels for 0%

commit v1 on v0

--- a/solution.py
+++ b/solution.py
@@ -71,7 +71,16 @@
         if iteration < ITERS - 1:
             cur_low = current.astype(jnp.bfloat16)
             iterate_rows = lax.all_gather(cur_low, "col", axis=1, tiled=True)
-            iterate_cols = lax.all_gather(cur_low, "row", axis=0, tiled=True)
+            ring = [cur_low]
+            for hop in range(7):
+                ring.append(
+                    lax.ppermute(ring[-1], "row", [(dev, (dev + 1) % 8) for dev in range(8)])
+                )
+            iterate_cols = jnp.roll(
+                jnp.concatenate(ring[::-1], axis=0),
+                (lax.axis_index("row") + 1) * ring[0].shape[0],
+                axis=0,
+            )
     summed = lax.psum(jnp.stack(partial_list), ("row", "col"))
     residual_norms = jnp.sqrt(summed / order)
     return (transpose_blocks(current, row_size, col_size), residual_norms)

time: 791 us -> 734 us (0.928)
  waiting for transfers between devices: 543 us -> 464 us
  local copies, waits for them, and re-layouts: 3.86 us -> 36.1 us
  blocking collectives: 152 us -> 139 us
    ppermute x0 -> x14, waiting for transfers between devices: none -> 310 us  [shards(): lax.ppermute(ring[-1], 'row', [(dev, (dev + 1) % 8) for dev in range(8)])]
    all_gather x2 -> x0, waiting for transfers between devices: 253 us -> none  [shards(): iterate_cols = lax.all_gather(cur_low, 'row', axis=0, tiled=True)]
    all_gather x3, waiting for transfers between devices: 101 us -> 32.7 us  [shards(): lax.all_gather(shift_low, 'col', axis=1, tiled=True)]
    all_gather x2, waiting for transfers between devices: 67.1 us -> 0.01 us  [shards(): iterate_rows = lax.all_gather(cur_low, 'col', axis=1, tiled=True)]
    unnamed x4 -> x28, local copies, waits for them, and re-layouts: 1.32 us -> 31.4 us
    psum x1, blocking collectives: 110 us -> 96.9 us  [shards(): summed = lax.psum(jnp.stack(partial_list), ('row', 'col'))]
  transfers between devices with their start and end apart: 11 -> 23, of which waited for: 8 -> 16; matrix products, arithmetic and copies ran while one was open for 1% -> 8% of each run, Pallas kernels for 0% -> 0%
where the time goes in v1:
time: 734 us; the launch traced here: 733 us
  waiting for transfers between devices  464 us (63%)
  blocking collectives  139 us (19%)
  matrix products  67 us (9%)
  local copies, waits for them, and re-layouts  36.1 us (5%)
  between operations  15.4 us (2%)
    ppermute x14, waiting for transfers between devices, shards(): lax.ppermute(ring[-1], 'row', [(dev, (dev + 1) % 8) for dev in range(8)])  310 us
    all_gather x1, waiting for transfers between devices, shards(): panel_cols = lax.all_gather(mat_low, 'row', axis=0, tiled=True)  120 us
    psum x1, blocking collectives, shards(): summed = lax.psum(jnp.stack(partial_list), ('row', 'col'))  96.9 us
    psum x1, blocking collectives, shards(): sq_total = lax.psum(jnp.sum(matrix * matrix), ('row', 'col'))  42.5 us
    dot_general x3, matrix products, shards(): jnp.dot(iterate_rows, panel_cols, preferred_element_type=jnp.float32)  36.2 us
    all_gather x3, waiting for transfers between devices, shards(): lax.all_gather(shift_low, 'col', axis=1, tiled=True)  32.7 us
    unnamed x28, local copies, waits for them, and re-layouts  31.4 us
    dot_general x3, matrix products, shards(): jnp.dot(lax.all_gather(shift_low, 'col', axis=1, tiled=True), iterate_col...  30.8 us
  transfers between devices with their start and end apart: 23, of which 16 were waited for; matrix products, arithmetic and copies ran while one was open for 8% of the time, Pallas kernels for 0%

profile of v1, /device:TPU:0, one launch (start us, length us, event | category | flops | bytes accessed | tf_op | source)
XLA Modules:
  0.0 732.9 jit_solution(14986204761664931840)
XLA Ops:
  7.2 0.0 all-gather.8.cloned.1.call-start
  7.2 4.3 multiply_reduce_fusion.3
  11.5 0.0 all-gather.10.cloned.1.call-start
  11.5 0.7 all-gather.10.cloned.1.call-update
  12.3 0.0 all-gather.12.cloned.1.call-start
  12.3 42.5 %psum.14 = f32[]{:T(128)} all-reduce(f32[]{:T(128)} %get-tuple-element.10), channel_id=1, replica_groups=mesh['row'=8,'col'=4] {'row','col'}, use_global_device_ids=true, to_apply=%region_1.0 | all-reduce | flops 1 | bytes 8 | tf_op jit(solution)/shard_map/psum | solution.py:52
  56.0 120.3 %all-gather.10.cloned.1.call-done = bf16[4096,1024]{1,0:T(8,128)(2,1)} async-done(((bf16[512,1024]{1,0:T(8,128)(2,1)}), bf16[4096,1024]{1,0:T(8,128)(2,1)}) %all-gather.10.cloned.1.call-update) | async-done | bytes 8388624 | tf_op jit(solution)/shard_map/all_gather | solution.py:54
  176.3 12.1 %fusion.18 = (bf16[512,1024]{1,0:T(8,128)(2,1)}, f32[512,1024]{1,0:T(8,128)}) fusion(s32[1024]{0:T(1024)S(1)} %iota_add_fusion, s32[512]{0:T(512)S(1)} %iota_add_fusion.1, bf16[4096,1024]{1,0:T(8,128)(2,1)} %all-gather.10.cloned.1.call-done, bf16[512,4096]{1,0:T(8,128)(2,1)} %all-gather.8.cloned.1.call-done, f32[]{:T(128)} %reduce_precision.12), kind=kOutput, calls=%fused_computation.29 | convolution fusion | flops 4316463104 | bytes 15734788 | tf_op jit(solution)/shard_map/dot_general | solution.py:62
  188.4 0.0 all-gather.14.cloned.1.call-start
  188.5 32.7 %all-gather.12.cloned.1.call-done = bf16[512,4096]{1,0:T(8,128)(2,1)} async-done(((bf16[512,1024]{1,0:T(8,128)(2,1)}), bf16[512,4096]{1,0:T(8,128)(2,1)}) %all-gather.12.cloned.1.call-update) | async-done | bytes 4194320 | tf_op jit(solution)/shard_map/all_gather | solution.py:67
  221.2 11.9 %fusion.23 = bf16[512,1024]{1,0:T(8,128)(2,1)} fusion(bf16[512,4096]{1,0:T(8,128)(2,1)} %all-gather.12.cloned.1.call-done, bf16[4096,1024]{1,0:T(8,128)(2,1)} %all-gather.10.cloned.1.call-done, s32[1024]{0:T(1024)S(1)} %iota_add_fusion, f32[]{:T(128)} %reduce_precision.12), kind=kOutput, calls=%fused_computation.38 | convolution fusion | flops 4333240320 | bytes 13635588 | tf_op jit(solution)/shard_map/dot_general | solution.py:66
  233.2 0.2 all-gather.16.cloned.1.call-start
  233.4 1.5 collective-permute-start
  234.9 26.7 %collective-permute-done = bf16[512,1024]{1,0:T(8,128)(2,1)S(1)} collective-permute-done((bf16[512,1024]{1,0:T(8,128)(2,1)}, bf16[512,1024]{1,0:T(8,128)(2,1)S(1)}, u32[]{:S(2)}, u32[]{:S(2)}) %collective-permute-start) | collective-permute-done | bytes 1048608 | tf_op jit(solution)/shard_map/ppermute | solution.py:77
  261.7 27.1 %collective-permute-done.1 = bf16[512,1024]{1,0:T(8,128)(2,1)S(1)} collective-permute-done((bf16[512,1024]{1,0:T(8,128)(2,1)S(1)}, bf16[512,1024]{1,0:T(8,128)(2,1)S(1)}, u32[]{:S(2)}, u32[]{:S(2)}) %collective-permute-start.1) | collective-permute-done | bytes 1048608 | tf_op jit(solution)/shard_map/ppermute | solution.py:77
  288.8 10.9 %fusion.19 = (bf16[512,1024]{1,0:T(8,128)(2,1)}, f32[512,1024]{1,0:T(8,128)}) fusion(s32[1024]{0:T(1024)S(1)} %iota_add_fusion, s32[512]{0:T(512)S(1)} %iota_add_fusion.1, bf16[512,4096]{1,0:T(8,128)(2,1)} %all-gather.14.cloned.1.call-done, bf16[4096,1024]{1,0:T(8,128)(2,1)} %all-gather.10.cloned.1.call-done), kind=kOutput, calls=%fused_computation.30 | convolution fusion | flops 4297588736 | bytes 15734784 | tf_op jit(solution)/shard_map/dot_general | solution.py:62
  299.8 0.0 all-gather.18.cloned.1.call-start
  299.9 15.4 %collective-permute-done.2 = bf16[512,1024]{1,0:T(8,128)(2,1)} collective-permute-done((bf16[512,1024]{1,0:T(8,128)(2,1)S(1)}, bf16[512,1024]{1,0:T(8,128)(2,1)}, u32[]{:S(2)}, u32[]{:S(2)}) %collective-permute-start.2) | collective-permute-done | bytes 1048608 | tf_op jit(solution)/shard_map/ppermute | solution.py:77
  315.2 25.6 %collective-permute-done.3 = bf16[512,1024]{1,0:T(8,128)(2,1)S(1)} collective-permute-done((bf16[512,1024]{1,0:T(8,128)(2,1)}, bf16[512,1024]{1,0:T(8,128)(2,1)S(1)}, u32[]{:S(2)}, u32[]{:S(2)}) %collective-permute-start.3) | collective-permute-done | bytes 1048608 | tf_op jit(solution)/shard_map/ppermute | solution.py:77
  340.9 1.0 copy-done.4
  341.9 24.6 %collective-permute-done.4 = bf16[512,1024]{1,0:T(8,128)(2,1)S(1)} collective-permute-done((bf16[512,1024]{1,0:T(8,128)(2,1)S(1)}, bf16[512,1024]{1,0:T(8,128)(2,1)S(1)}, u32[]{:S(2)}, u32[]{:S(2)}) %collective-permute-start.4) | collective-permute-done | bytes 1048608 | tf_op jit(solution)/shard_map/ppermute | solution.py:77
  366.5 1.0 copy-done.6
  367.4 23.8 %collective-permute-done.5 = bf16[512,1024]{1,0:T(8,128)(2,1)} collective-permute-done((bf16[512,1024]{1,0:T(8,128)(2,1)S(1)}, bf16[512,1024]{1,0:T(8,128)(2,1)}, u32[]{:S(2)}, u32[]{:S(2)}) %collective-permute-start.5) | collective-permute-done | bytes 1048608 | tf_op jit(solution)/shard_map/ppermute | solution.py:77
  391.3 23.2 %collective-permute-done.6 = bf16[512,1024]{1,0:T(8,128)(2,1)} collective-permute-done((bf16[512,1024]{1,0:T(8,128)(2,1)}, bf16[512,1024]{1,0:T(8,128)(2,1)}, u32[]{:S(2)}, u32[]{:S(2)}) %collective-permute-start.6) | collective-permute-done | bytes 1048608 | tf_op jit(solution)/shard_map/ppermute | solution.py:77
  414.4 2.4 constant_dynamic-update-slice_fusion.7
  416.8 2.3 constant_dynamic-update-slice_fusion.6
  419.1 2.3 constant_dynamic-update-slice_fusion.5
  421.4 2.3 constant_dynamic-update-slice_fusion.4
  423.7 2.3 constant_dynamic-update-slice_fusion.3
  426.0 1.0 constant_dynamic-update-slice_fusion.2
  427.0 1.1 constant_dynamic-update-slice_fusion.1
  428.1 1.1 constant_dynamic-update-slice_fusion
  429.2 10.6 %fusion.26 = bf16[512,1024]{1,0:T(8,128)(2,1)} fusion(bf16[512,4096]{1,0:T(8,128)(2,1)} %all-gather.16.cloned.1.call-done, s32[]{:T(128)S(6)} %select_n.26, bf16[4096,1024]{1,0:T(8,128)(2,1)} %constant_dynamic-update-slice_fusion), kind=kOutput, calls=%fused_computation.39 | convolution fusion | flops 4312268800 | bytes 13631492 | tf_op jit(solution)/shard_map/dot_general | solution.py:66
  439.7 0.0 all-gather.20.cloned.1.call-start
  439.8 0.1 collective-permute-start.7
  439.8 23.5 %collective-permute-done.7 = bf16[512,1024]{1,0:T(8,128)(2,1)S(1)} collective-permute-done((bf16[512,1024]{1,0:T(8,128)(2,1)}, bf16[512,1024]{1,0:T(8,128)(2,1)S(1)}, u32[]{:S(2)}, u32[]{:S(2)}) %collective-permute-start.7) | collective-permute-done | bytes 1048608 | tf_op jit(solution)/shard_map/ppermute | solution.py:77
  463.4 23.1 %collective-permute-done.8 = bf16[512,1024]{1,0:T(8,128)(2,1)} collective-permute-done((bf16[512,1024]{1,0:T(8,128)(2,1)S(1)}, bf16[512,1024]{1,0:T(8,128)(2,1)}, u32[]{:S(2)}, u32[]{:S(2)}) %collective-permute-start.8) | collective-permute-done | bytes 1048608 | tf_op jit(solution)/shard_map/ppermute | solution.py:77
  486.5 13.1 %fusion.22 = (f32[]{:T(128)}, f32[]{:T(128)}, f32[]{:T(128)}, f32[]{:T(128)}, bf16[512,1024]{1,0:T(8,128)(2,1)}) fusion(f32[512,1024]{1,0:T(8,128)S(1)} %copy-done.3, f32[]{:T(128)} %reduce_precision.12, s32[1024]{0:T(1024)S(1)} %iota_add_fusion, s32[512]{0:T(512)S(1)} %iota_add_fusion.1, f32[512,1024]{1,0:T(8,128)} %get-tuple-element.15, ...), kind=kOutput, calls=%fused_computation.33 | convolution fusion | flops 4304404480 | bytes 19929108 | tf_op jit(solution)/shard_map/dot_general | solution.py:62
  499.6 10.2 %collective-permute-done.9 = bf16[512,1024]{1,0:T(8,128)(2,1)} collective-permute-done((bf16[512,1024]{1,0:T(8,128)(2,1)}, bf16[512,1024]{1,0:T(8,128)(2,1)}, u32[]{:S(2)}, u32[]{:S(2)}) %collective-permute-start.9) | collective-permute-done | bytes 1048608 | tf_op jit(solution)/shard_map/ppermute | solution.py:77
  509.8 23.5 %collective-permute-done.10 = bf16[512,1024]{1,0:T(8,128)(2,1)S(1)} collective-permute-done((bf16[512,1024]{1,0:T(8,128)(2,1)}, bf16[512,1024]{1,0:T(8,128)(2,1)S(1)}, u32[]{:S(2)}, u32[]{:S(2)}) %collective-permute-start.10) | collective-permute-done | bytes 1048608 | tf_op jit(solution)/shard_map/ppermute | solution.py:77
  533.3 22.4 %collective-permute-done.11 = bf16[512,1024]{1,0:T(8,128)(2,1)S(1)} collective-permute-done((bf16[512,1024]{1,0:T(8,128)(2,1)S(1)}, bf16[512,1024]{1,0:T(8,128)(2,1)S(1)}, u32[]{:S(2)}, u32[]{:S(2)}) %collective-permute-start.11) | collective-permute-done | bytes 1048608 | tf_op jit(solution)/shard_map/ppermute | solution.py:77
  555.7 1.0 copy-done.5
  556.7 23.1 %collective-permute-done.12 = bf16[512,1024]{1,0:T(8,128)(2,1)} collective-permute-done((bf16[512,1024]{1,0:T(8,128)(2,1)S(1)}, bf16[512,1024]{1,0:T(8,128)(2,1)}, u32[]{:S(2)}, u32[]{:S(2)}) %collective-permute-start.12) | collective-permute-done | bytes 1048608 | tf_op jit(solution)/shard_map/ppermute | solution.py:77
  579.8 17.8 %collective-permute-done.13 = bf16[512,1024]{1,0:T(8,128)(2,1)} collective-permute-done((bf16[512,1024]{1,0:T(8,128)(2,1)}, bf16[512,1024]{1,0:T(8,128)(2,1)}, u32[]{:S(2)}, u32[]{:S(2)}) %collective-permute-start.13) | collective-permute-done | bytes 1048608 | tf_op jit(solution)/shard_map/ppermute | solution.py:77
  597.6 2.3 constant_dynamic-update-slice_fusion.15
  599.9 2.3 constant_dynamic-update-slice_fusion.14
  602.2 2.3 constant_dynamic-update-slice_fusion.13
  604.4 1.0 constant_dynamic-update-slice_fusion.12
  605.5 2.3 constant_dynamic-update-slice_fusion.11
  607.8 2.3 constant_dynamic-update-slice_fusion.10
  610.0 1.0 constant_dynamic-update-slice_fusion.9
  611.1 1.2 constant_dynamic-update-slice_fusion.8
  612.2 8.4 %fusion.7 = f32[512,1024]{1,0:T(8,128)S(1)} fusion(bf16[512,4096]{1,0:T(8,128)(2,1)} %all-gather.20.cloned.1.call-done, s32[]{:T(128)S(6)} %select_n.26, bf16[4096,1024]{1,0:T(8,128)(2,1)} %constant_dynamic-update-slice_fusion.8), kind=kOutput, calls=%fused_computation.14 | convolution fusion | flops 4311744512 | bytes 14680068 | tf_op jit(solution)/shard_map/dot_general | solution.py:66
  620.6 0.2 constant_dynamic-slice_fusion
  620.8 1.7 collective-permute-start.14
  622.5 2.5 pad_maximum_fusion
  624.9 96.9 %psum.15 = f32[4]{0:T(128)S(1)} all-reduce(f32[4]{0:T(128)S(1)} %pad_maximum_fusion), channel_id=1, replica_groups=mesh['row'=8,'col'=4] {'row','col'}, use_global_device_ids=true, to_apply=%region_6.8 | all-reduce | flops 4 | bytes 32 | tf_op jit(solution)/shard_map/psum | solution.py:84
  721.8 0.5 multiply_sqrt_fusion
  722.4 1.6 copy.3
  723.9 0.3 copy.4
  724.3 0.2 broadcast_in_dim.3
  724.5 0.1 constant_dynamic-update-slice_fusion.17
  724.6 0.1 constant_dynamic-update-slice_fusion.16
  724.7 1.3 copy-done.2
  (38 shorter events, 0.2 us)
Async XLA Ops:
  7.2 48.9 %all-gather.8.cloned.1.call-start = ((), (), s32[]{:S(2)}) async-start(), calls=%async_computation | async-start | bytes 5242880 | tf_op jit(solution)/shard_map/all_gather | solution.py:53
  11.5 164.8 %all-gather.10.cloned.1.call-start = ((), (), s32[]{:S(2)}) async-start(), calls=%async_computation.1 | async-start | bytes 9437184 | tf_op jit(solution)/shard_map/all_gather | solution.py:54
  12.3 209.0 %all-gather.12.cloned.1.call-start = ((), (), s32[]{:S(2)}) async-start(), calls=%async_computation.2 | async-start | bytes 5242880 | tf_op jit(solution)/shard_map/all_gather | solution.py:67
  188.4 100.4 %all-gather.14.cloned.1.call-start = ((), (), s32[]{:S(2)}) async-start(), calls=%async_computation.3 | async-start | bytes 5242880 | tf_op jit(solution)/shard_map/all_gather | solution.py:73
  233.2 196.0 %all-gather.16.cloned.1.call-start = ((), (), s32[]{:S(2)}) async-start(), calls=%async_computation.4 | async-start | bytes 5242880 | tf_op jit(solution)/shard_map/all_gather | solution.py:67
  233.4 28.3 %collective-permute-start = (bf16[512,1024]{1,0:T(8,128)(2,1)}, bf16[512,1024]{1,0:T(8,128)(2,1)S(1)}, u32[]{:S(2)}, u32[]{:S(2)}) collective-permute-start(bf16[512,1024]{1,0:T(8,128)(2,1)} %fusion.23), channel_id=1, source_target_pairs={{0,4},{4,8},{8,12},{12,16},{16,20},{20,24},{24,28},{28,0},{1,5},{5... | collective-permute-start | bytes 3145736 | tf_op jit(solution)/shard_map/ppermute | solution.py:77
  261.7 27.1 %collective-permute-start.1 = (bf16[512,1024]{1,0:T(8,128)(2,1)S(1)}, bf16[512,1024]{1,0:T(8,128)(2,1)S(1)}, u32[]{:S(2)}, u32[]{:S(2)}) collective-permute-start(bf16[512,1024]{1,0:T(8,128)(2,1)S(1)} %collective-permute-done), channel_id=1, source_target_pairs={{0,4},{4,8},{8,12},{12,16},{16,20},{20,24},{24,28},{28,0},{1,5},{5... | collective-permute-start | bytes 3145736 | tf_op jit(solution)/shard_map/ppermute | solution.py:77
  288.8 26.4 %collective-permute-start.2 = (bf16[512,1024]{1,0:T(8,128)(2,1)S(1)}, bf16[512,1024]{1,0:T(8,128)(2,1)}, u32[]{:S(2)}, u32[]{:S(2)}) collective-permute-start(bf16[512,1024]{1,0:T(8,128)(2,1)S(1)} %collective-permute-done.1), channel_id=1, source_target_pairs={{0,4},{4,8},{8,12},{12,16},{16,20},{20,24},{24,28},{28,0},{1,5},{5... | collective-permute-start | bytes 3145736 | tf_op jit(solution)/shard_map/ppermute | solution.py:77
  299.8 128.3 %copy-start.1 = (bf16[512,1024]{1,0:T(8,128)(2,1)S(1)}, bf16[512,1024]{1,0:T(8,128)(2,1)}, u32[]{:S(2)}) copy-start(bf16[512,1024]{1,0:T(8,128)(2,1)} %fusion.23) | copy-start | bytes 3145732
  299.8 186.7 %all-gather.18.cloned.1.call-start = ((), (), s32[]{:S(2)}) async-start(), calls=%async_computation.5 | async-start | bytes 5242880 | tf_op jit(solution)/shard_map/all_gather | solution.py:73
  315.2 25.6 %collective-permute-start.3 = (bf16[512,1024]{1,0:T(8,128)(2,1)}, bf16[512,1024]{1,0:T(8,128)(2,1)S(1)}, u32[]{:S(2)}, u32[]{:S(2)}) collective-permute-start(bf16[512,1024]{1,0:T(8,128)(2,1)} %collective-permute-done.2), channel_id=1, source_target_pairs={{0,4},{4,8},{8,12},{12,16},{16,20},{20,24},{24,28},{28,0},{1,5},{5... | collective-permute-start | bytes 3145736 | tf_op jit(solution)/shard_map/ppermute | solution.py:77
  340.9 1.0 copy-start.4
  341.9 24.6 %collective-permute-start.4 = (bf16[512,1024]{1,0:T(8,128)(2,1)S(1)}, bf16[512,1024]{1,0:T(8,128)(2,1)S(1)}, u32[]{:S(2)}, u32[]{:S(2)}) collective-permute-start(bf16[512,1024]{1,0:T(8,128)(2,1)S(1)} %collective-permute-done.3), channel_id=1, source_target_pairs={{0,4},{4,8},{8,12},{12,16},{16,20},{20,24},{24,28},{28,0},{1,5},{5... | collective-permute-start | bytes 3145736 | tf_op jit(solution)/shard_map/ppermute | solution.py:77
  366.5 1.0 copy-start.6
  367.4 23.8 %collective-permute-start.5 = (bf16[512,1024]{1,0:T(8,128)(2,1)S(1)}, bf16[512,1024]{1,0:T(8,128)(2,1)}, u32[]{:S(2)}, u32[]{:S(2)}) collective-permute-start(bf16[512,1024]{1,0:T(8,128)(2,1)S(1)} %collective-permute-done.4), channel_id=1, source_target_pairs={{0,4},{4,8},{8,12},{12,16},{16,20},{20,24},{24,28},{28,0},{1,5},{5... | collective-permute-start | bytes 3145736 | tf_op jit(solution)/shard_map/ppermute | solution.py:77
  391.3 23.2 %collective-permute-start.6 = (bf16[512,1024]{1,0:T(8,128)(2,1)}, bf16[512,1024]{1,0:T(8,128)(2,1)}, u32[]{:S(2)}, u32[]{:S(2)}) collective-permute-start(bf16[512,1024]{1,0:T(8,128)(2,1)} %collective-permute-done.5), channel_id=1, source_target_pairs={{0,4},{4,8},{8,12},{12,16},{16,20},{20,24},{24,28},{28,0},{1,5},{5... | collective-permute-start | bytes 3145736 | tf_op jit(solution)/shard_map/ppermute | solution.py:77
  429.1 57.3 %copy-start.3 = (f32[512,1024]{1,0:T(8,128)S(1)}, f32[512,1024]{1,0:T(8,128)}, u32[]{:S(2)}) copy-start(f32[512,1024]{1,0:T(8,128)} %param.3) | copy-start | bytes 6291460
  439.7 172.5 %all-gather.20.cloned.1.call-start = ((), (), s32[]{:S(2)}) async-start(), calls=%async_computation.6 | async-start | bytes 5242880 | tf_op jit(solution)/shard_map/all_gather | solution.py:67
  439.8 23.6 %collective-permute-start.7 = (bf16[512,1024]{1,0:T(8,128)(2,1)}, bf16[512,1024]{1,0:T(8,128)(2,1)S(1)}, u32[]{:S(2)}, u32[]{:S(2)}) collective-permute-start(bf16[512,1024]{1,0:T(8,128)(2,1)} %fusion.26), channel_id=1, source_target_pairs={{0,4},{4,8},{8,12},{12,16},{16,20},{20,24},{24,28},{28,0},{1,5},{5... | collective-permute-start | bytes 3145736 | tf_op jit(solution)/shard_map/ppermute | solution.py:77
  463.4 23.1 %collective-permute-start.8 = (bf16[512,1024]{1,0:T(8,128)(2,1)S(1)}, bf16[512,1024]{1,0:T(8,128)(2,1)}, u32[]{:S(2)}, u32[]{:S(2)}) collective-permute-start(bf16[512,1024]{1,0:T(8,128)(2,1)S(1)} %collective-permute-done.7), channel_id=1, source_target_pairs={{0,4},{4,8},{8,12},{12,16},{16,20},{20,24},{24,28},{28,0},{1,5},{5... | collective-permute-start | bytes 3145736 | tf_op jit(solution)/shard_map/ppermute | solution.py:77
  486.5 23.3 %collective-permute-start.9 = (bf16[512,1024]{1,0:T(8,128)(2,1)}, bf16[512,1024]{1,0:T(8,128)(2,1)}, u32[]{:S(2)}, u32[]{:S(2)}) collective-permute-start(bf16[512,1024]{1,0:T(8,128)(2,1)} %collective-permute-done.8), channel_id=1, source_target_pairs={{0,4},{4,8},{8,12},{12,16},{16,20},{20,24},{24,28},{28,0},{1,5},{5... | collective-permute-start | bytes 3145736 | tf_op jit(solution)/shard_map/ppermute | solution.py:77
  499.6 111.5 %copy-start = (bf16[512,1024]{1,0:T(8,128)(2,1)S(1)}, bf16[512,1024]{1,0:T(8,128)(2,1)}, u32[]{:S(2)}) copy-start(bf16[512,1024]{1,0:T(8,128)(2,1)} %fusion.26) | copy-start | bytes 3145732
  509.8 23.5 %collective-permute-start.10 = (bf16[512,1024]{1,0:T(8,128)(2,1)}, bf16[512,1024]{1,0:T(8,128)(2,1)S(1)}, u32[]{:S(2)}, u32[]{:S(2)}) collective-permute-start(bf16[512,1024]{1,0:T(8,128)(2,1)} %collective-permute-done.9), channel_id=1, source_target_pairs={{0,4},{4,8},{8,12},{12,16},{16,20},{20,24},{24,28},{28,0},{1,5},{5... | collective-permute-start | bytes 3145736 | tf_op jit(solution)/shard_map/ppermute | solution.py:77
  533.3 22.4 %collective-permute-start.11 = (bf16[512,1024]{1,0:T(8,128)(2,1)S(1)}, bf16[512,1024]{1,0:T(8,128)(2,1)S(1)}, u32[]{:S(2)}, u32[]{:S(2)}) collective-permute-start(bf16[512,1024]{1,0:T(8,128)(2,1)S(1)} %collective-permute-done.10), channel_id=1, source_target_pairs={{0,4},{4,8},{8,12},{12,16},{16,20},{20,24},{24,28},{28,0},{1,5},{5... | collective-permute-start | bytes 3145736 | tf_op jit(solution)/shard_map/ppermute | solution.py:77
  555.7 1.0 copy-start.5
  556.7 23.1 %collective-permute-start.12 = (bf16[512,1024]{1,0:T(8,128)(2,1)S(1)}, bf16[512,1024]{1,0:T(8,128)(2,1)}, u32[]{:S(2)}, u32[]{:S(2)}) collective-permute-start(bf16[512,1024]{1,0:T(8,128)(2,1)S(1)} %collective-permute-done.11), channel_id=1, source_target_pairs={{0,4},{4,8},{8,12},{12,16},{16,20},{20,24},{24,28},{28,0},{1,5},{5... | collective-permute-start | bytes 3145736 | tf_op jit(solution)/shard_map/ppermute | solution.py:77
  579.8 17.8 %collective-permute-start.13 = (bf16[512,1024]{1,0:T(8,128)(2,1)}, bf16[512,1024]{1,0:T(8,128)(2,1)}, u32[]{:S(2)}, u32[]{:S(2)}) collective-permute-start(bf16[512,1024]{1,0:T(8,128)(2,1)} %collective-permute-done.12), channel_id=1, source_target_pairs={{0,4},{4,8},{8,12},{12,16},{16,20},{20,24},{24,28},{28,0},{1,5},{5... | collective-permute-start | bytes 3145736 | tf_op jit(solution)/shard_map/ppermute | solution.py:77
  620.8 101.6 %collective-permute-start.14 = (f32[512,512]{1,0:T(8,128)S(1)}, f32[512,512]{1,0:T(8,128)}, u32[]{:S(2)}, u32[]{:S(2)}) collective-permute-start(f32[512,512]{1,0:T(8,128)S(1)} %get-tuple-element.9), channel_id=1, source_target_pairs={{0,0},{1,8},{2,16},{3,24},{4,4},{5,12},{6,20},{7,28},{8,1},{9,9},{... | collective-permute-start | bytes 3145736 | tf_op jit(solution)/shard_map/ppermute | solution.py:34
  622.5 101.4 %collective-permute-start.15 = (f32[512,512]{1,0:T(8,128)S(1)}, f32[512,512]{1,0:T(8,128)S(1)}, u32[]{:S(2)}, u32[]{:S(2)}) collective-permute-start(f32[512,512]{1,0:T(8,128)S(1)} %get-tuple-element.8), channel_id=1, source_target_pairs={{0,4},{1,12},{2,20},{3,28},{4,0},{5,8},{6,16},{7,24},{8,5},{9,13},... | collective-permute-start | bytes 3145736 | tf_op jit(solution)/shard_map/ppermute | solution.py:34
  724.7 1.3 copy-start.2
Sparse Core Ops, SparseCore 0:
  11.6 37.4 all-gather.7
  51.8 124.4 all-gather.9
  188.6 32.6 all-gather.11
  233.3 34.4 all-gather.13
  299.9 34.9 all-gather.15
  439.8 30.5 all-gather.17
  499.8 34.9 all-gather.19
